TPU v7x, 32 devices: a whole 2x2x4 slice. The times are simulated.
32 devices in a mesh: dp: 8 (over z, core), tensor: 4 (over y, x).
Axes of the slice: x: 2, y: 2, z: 4, core: 2. Of those that a mesh axis runs over, the one named last changes fastest.
Arguments:
- block_input: bfloat16 [4096, 2048], P('dp'), may hold values from -6 to 6
- cotangent: bfloat16 [4096, 2048], P('dp'), may hold values from -6 to 6
- lengths: int32 [8], P('dp'), may hold values from 1 to 512, as said below
- attn_gain: bfloat16 [2048], P('dp'), may hold values from 0.5 to 1.5
- attn_shift: bfloat16 [2048], P('dp'), may hold values from -3 to 3
- ffn_gain: bfloat16 [2048], P('dp'), may hold values from 0.5 to 1.5
- ffn_shift: bfloat16 [2048], P('dp'), may hold values from -3 to 3
- qkv_weight: bfloat16 [3, 2048, 2048], P(None, 'dp', 'tensor')
- qkv_bias: bfloat16 [3, 2048], P(None, ('tensor', 'dp')), may hold values from -3 to 3
- out_weight: bfloat16 [2048, 2048], P('tensor', 'dp'), may hold values from -1 to 1
- out_bias: bfloat16 [2048], P('dp'), may hold values from -3 to 3
- up_weight: bfloat16 [2048, 8192], P('dp', 'tensor'), may hold values from -0.125 to 0.125
- up_bias: bfloat16 [8192], P(('tensor', 'dp')), may hold values from -3 to 3
- down_weight: bfloat16 [8192, 2048], P('tensor', 'dp'), may hold values from -0.0625 to 0.0625
Outputs:
- block_output: bfloat16 [4096, 2048], P('dp')
- dblock_input: bfloat16 [4096, 2048], P('dp')
- dattn_gain: float32 [2048], P('dp')
- dattn_shift: float32 [2048], P('dp')
- dffn_gain: float32 [2048], P('dp')
- dffn_shift: float32 [2048], P('dp')
- dqkv_weight: float32 [3, 2048, 2048], P(None, 'dp', 'tensor')
- dqkv_bias: float32 [3, 2048], P(None, ('tensor', 'dp'))
- dout_weight: float32 [2048, 2048], P('tensor', 'dp')
- dout_bias: float32 [2048], P('dp')
- dup_weight: float32 [2048, 8192], P('dp', 'tensor')
- dup_bias: float32 [8192], P(('tensor', 'dp'))
- ddown_weight: float32 [8192, 2048], P('tensor', 'dp')
Inputs may be any that keep to these rules, and one draw needn't show every extreme that they name: `lengths`: one sequence for each index of dp; some sequence uses all 512 slots.
All inputs are finite; a program needn't handle non-finite values.
Results may differ from a plain program's by a relative error of at most 0.014.
Values may be sent and summed in bfloat16 or wider, within the bound.
A program may use at most 192 MiB of HBM per device.

v0:
```python
import math
import jax
import jax.numpy as jnp
from jax import lax
from jax.sharding import PartitionSpec as P

HD = 256
ROT = 64
norm_eps = 1e-05
rope_base = 10000.0


def rope_tables(row_count, rot_width):
    half_rot = rot_width // 2
    freq_idx = jnp.arange(half_rot, dtype=jnp.float32)
    inv_freq = jnp.exp(-(2.0 * freq_idx / rot_width) * math.log(rope_base))
    angles = jnp.arange(row_count, dtype=jnp.float32)[:, None] * inv_freq[None, :]
    return (jnp.cos(angles), jnp.sin(angles))


def rotate(heads_arr, cosine, sine_tab, direction):
    half_rot = ROT // 2
    first_half = heads_arr[..., :half_rot]
    second_half = heads_arr[..., half_rot:ROT]
    rest_dims = heads_arr[..., ROT:]
    cos_b = cosine[:, None, :]
    sin_b = sine_tab[:, None, :] * direction
    new_first = first_half * cos_b - second_half * sin_b
    new_second = second_half * cos_b + first_half * sin_b
    return jnp.concatenate([new_first, new_second, rest_dims], axis=-1)


def gelu_exact(pre_act):
    return 0.5 * pre_act * (1.0 + lax.erf(pre_act * (1.0 / math.sqrt(2.0))))


def gelu_slope(pre_act):
    cdf_part = 0.5 * (1.0 + lax.erf(pre_act * (1.0 / math.sqrt(2.0))))
    return cdf_part + pre_act * jnp.exp(-0.5 * pre_act * pre_act) * (1.0 / math.sqrt(2.0 * math.pi))


def per_device(
    block_input,
    cotangent,
    lengths,
    attn_gain,
    attn_shift,
    ffn_gain,
    ffn_shift,
    qkv_weight,
    qkv_bias,
    out_weight,
    out_bias,
    up_weight,
    up_bias,
    down_weight,
):
    gathered = (
        lax.all_gather(qkv_weight, "dp", axis=1, tiled=True),
        lax.all_gather(out_weight, "dp", axis=1, tiled=True),
        lax.all_gather(up_weight, "dp", axis=0, tiled=True),
        lax.all_gather(down_weight, "dp", axis=1, tiled=True),
        lax.all_gather(qkv_bias, "dp", axis=1, tiled=True),
        lax.all_gather(up_bias, "dp", axis=0, tiled=True),
        lax.all_gather(out_bias, "dp", axis=0, tiled=True),
        lax.all_gather(attn_gain, "dp", axis=0, tiled=True),
        lax.all_gather(attn_shift, "dp", axis=0, tiled=True),
        lax.all_gather(ffn_gain, "dp", axis=0, tiled=True),
        lax.all_gather(ffn_shift, "dp", axis=0, tiled=True),
    )
    (
        qkv_full,
        out_full,
        up_full,
        down_full,
        qkv_b,
        up_b,
        outb_full,
        gain_a,
        shift_a,
        gain_f,
        shift_f,
    ) = gathered
    gain_a = gain_a.astype(jnp.float32)
    gain_f = gain_f.astype(jnp.float32)
    seq_rows = block_input.shape[0]
    local_width = qkv_full.shape[2]
    local_heads = local_width // HD
    seq_len = lengths[0]
    positions = jnp.arange(seq_rows, dtype=jnp.int32)
    scale_qk = 1.0 / math.sqrt(HD)
    block_rows = min(512, seq_rows)
    x_rows = block_input.astype(jnp.float32)
    row_mean = jnp.mean(x_rows, axis=-1, keepdims=True)
    centered = x_rows - row_mean
    inv_std = lax.rsqrt(jnp.mean(centered * centered, axis=-1, keepdims=True) + norm_eps)
    normed = centered * inv_std
    attn_in = (normed * gain_a + shift_a.astype(jnp.float32)).astype(jnp.bfloat16)
    ffn_in = (normed * gain_f + shift_f.astype(jnp.float32)).astype(jnp.bfloat16)
    qkv_rows = (
        jnp.einsum("ld,pde->ple", attn_in, qkv_full, preferred_element_type=jnp.float32)
        + qkv_b.astype(jnp.float32)[:, None, :]
    )
    cosine, sine_tab = rope_tables(seq_rows, ROT)
    query_rows = rotate(
        qkv_rows[0].reshape(seq_rows, local_heads, HD), cosine, sine_tab, 1.0
    ).astype(jnp.bfloat16)
    key_rows = rotate(qkv_rows[1].reshape(seq_rows, local_heads, HD), cosine, sine_tab, 1.0).astype(
        jnp.bfloat16
    )
    value_rows = qkv_rows[2].reshape(seq_rows, local_heads, HD).astype(jnp.bfloat16)

    def block_scores(row_lo, key_end):
        raw_scores = (
            jnp.einsum("lhe,mhe->hlm", query_rows, key_rows, preferred_element_type=jnp.float32)
            * scale_qk
        )
        key_mask = (positions[None, :key_end] <= positions[row_lo:key_end, None]) & (
            positions[None, :key_end] < seq_len
        )
        return jnp.where(key_mask[None], raw_scores, -jnp.inf)

    qblock = 0
    row_lo = qblock * block_rows
    key_end = row_lo + block_rows
    scores = block_scores(row_lo, key_end)
    row_max = jnp.max(scores, axis=-1, keepdims=True)
    exp_terms = jnp.exp(scores - row_max)
    row_total = jnp.sum(exp_terms, axis=-1, keepdims=True)
    prob_bf = (exp_terms / row_total).astype(jnp.bfloat16)
    lse_blocks = [row_max + jnp.log(row_total)]
    attn_blocks = jnp.einsum(
        "hlm,mhe->lhe", prob_bf, value_rows, preferred_element_type=jnp.float32
    ).astype(jnp.bfloat16)
    mixed_flat = attn_blocks.reshape(seq_rows, local_width)
    attn_part = jnp.dot(mixed_flat, out_full, preferred_element_type=jnp.float32)
    up_pre = jnp.dot(ffn_in, up_full, preferred_element_type=jnp.float32) + up_b.astype(jnp.float32)
    hidden = gelu_exact(up_pre).astype(jnp.bfloat16)
    ffn_part = jnp.dot(hidden, down_full, preferred_element_type=jnp.float32)
    branch_sum = lax.psum(attn_part + ffn_part, "tensor")
    block_output = (x_rows + branch_sum + outb_full.astype(jnp.float32)).astype(jnp.bfloat16)
    qkv_back, out_back, up_back, down_back = (qkv_full, out_full, up_full, down_full)
    row_valid = (positions < seq_len).astype(jnp.float32)[:, None]
    grad_rows = cotangent.astype(jnp.float32) * row_valid
    grad_bf = grad_rows.astype(jnp.bfloat16)
    dout_b = jnp.sum(grad_rows, axis=0)
    ddown_w = jnp.einsum("lf,ld->fd", hidden, grad_bf, preferred_element_type=jnp.float32)
    up_grad32 = jnp.einsum(
        "ld,fd->lf", grad_bf, down_back, preferred_element_type=jnp.float32
    ) * gelu_slope(up_pre)
    up_grad = up_grad32.astype(jnp.bfloat16)
    dup_w = jnp.einsum("ld,lf->df", ffn_in, up_grad, preferred_element_type=jnp.float32)
    dup_b = jnp.sum(up_grad32, axis=0)
    ffn_back = jnp.einsum("lf,df->ld", up_grad, up_back, preferred_element_type=jnp.float32)
    mixed_grad = (
        jnp.einsum("ld,ed->le", grad_bf, out_back, preferred_element_type=jnp.float32)
        .astype(jnp.bfloat16)
        .reshape(seq_rows, local_heads, HD)
    )
    dout_w = jnp.einsum("le,ld->ed", mixed_flat, grad_bf, preferred_element_type=jnp.float32)
    delta_rows = jnp.einsum(
        "lhe,lhe->hl", mixed_grad, attn_blocks, preferred_element_type=jnp.float32
    )
    query_grad = jnp.zeros((seq_rows, local_heads, HD), jnp.float32)
    key_grad = jnp.zeros((seq_rows, local_heads, HD), jnp.float32)
    value_grad = jnp.zeros((seq_rows, local_heads, HD), jnp.float32)
    qblock = 0
    row_lo = qblock * block_rows
    key_end = row_lo + block_rows
    scores = block_scores(row_lo, key_end)
    probs32 = jnp.exp(scores - lse_blocks[qblock])
    prob_back = probs32.astype(jnp.bfloat16)
    value_grad = value_grad.at[:key_end].add(
        jnp.einsum("hlm,lhe->mhe", prob_back, mixed_grad, preferred_element_type=jnp.float32)
    )
    prob_grad = jnp.einsum(
        "lhe,mhe->hlm", mixed_grad, value_rows, preferred_element_type=jnp.float32
    )
    score_grad = (probs32 * (prob_grad - delta_rows[:, row_lo:key_end, None]) * scale_qk).astype(
        jnp.bfloat16
    )
    query_grad = query_grad.at[row_lo:key_end].set(
        jnp.einsum("hlm,mhe->lhe", score_grad, key_rows, preferred_element_type=jnp.float32)
    )
    key_grad = key_grad.at[:key_end].add(
        jnp.einsum("hlm,lhe->mhe", score_grad, query_rows, preferred_element_type=jnp.float32)
    )
    query_grad = rotate(query_grad, cosine, sine_tab, -1.0)
    key_grad = rotate(key_grad, cosine, sine_tab, -1.0)
    qkv_grad32 = jnp.stack([query_grad, key_grad, value_grad]).reshape(3, seq_rows, local_width)
    dqkv_b = jnp.sum(qkv_grad32, axis=1)
    qkv_grad = qkv_grad32.astype(jnp.bfloat16)
    dqkv_w = jnp.einsum("ld,ple->pde", attn_in, qkv_grad, preferred_element_type=jnp.float32)
    attn_back = jnp.einsum("ple,pde->ld", qkv_grad, qkv_back, preferred_element_type=jnp.float32)
    norm_part = attn_back * gain_a + ffn_back * gain_f
    norm_stats = jnp.stack(
        [
            jnp.sum(attn_back * normed, axis=0),
            jnp.sum(attn_back, axis=0),
            jnp.sum(ffn_back * normed, axis=0),
            jnp.sum(ffn_back, axis=0),
        ]
    )
    norm_grad, stat_sum = lax.psum((norm_part, norm_stats), "tensor")
    grad_mean = jnp.mean(norm_grad, axis=-1, keepdims=True)
    grad_proj = jnp.mean(norm_grad * normed, axis=-1, keepdims=True)
    dblock_input = (grad_rows + inv_std * (norm_grad - grad_mean - normed * grad_proj)).astype(
        jnp.bfloat16
    )
    dqkv_sent, dout_sent, dup_sent, ddown_sent, dqkvb_sent, dupb_sent, doutb_sent, stats_sent = (
        lax.psum_scatter(dqkv_w, "dp", scatter_dimension=1, tiled=True),
        lax.psum_scatter(dout_w, "dp", scatter_dimension=1, tiled=True),
        lax.psum_scatter(dup_w, "dp", scatter_dimension=0, tiled=True),
        lax.psum_scatter(ddown_w, "dp", scatter_dimension=1, tiled=True),
        lax.psum_scatter(dqkv_b, "dp", scatter_dimension=1, tiled=True),
        lax.psum_scatter(dup_b, "dp", scatter_dimension=0, tiled=True),
        lax.psum_scatter(dout_b, "dp", scatter_dimension=0, tiled=True),
        lax.psum_scatter(stat_sum, "dp", scatter_dimension=1, tiled=True),
    )
    return (
        block_output,
        dblock_input,
        stats_sent[0],
        stats_sent[1],
        stats_sent[2],
        stats_sent[3],
        dqkv_sent,
        dqkvb_sent,
        dout_sent,
        doutb_sent,
        dup_sent,
        dupb_sent,
        ddown_sent,
    )


def solution(mesh):
    in_specs = (
        P("dp", None),
        P("dp", None),
        P("dp"),
        P("dp"),
        P("dp"),
        P("dp"),
        P("dp"),
        P(None, "dp", "tensor"),
        P(None, ("tensor", "dp")),
        P("tensor", "dp"),
        P("dp"),
        P("dp", "tensor"),
        P(("tensor", "dp")),
        P("tensor", "dp"),
    )
    out_specs = (
        P("dp", None),
        P("dp", None),
        P("dp"),
        P("dp"),
        P("dp"),
        P("dp"),
        P(None, "dp", "tensor"),
        P(None, ("tensor", "dp")),
        P("tensor", "dp"),
        P("dp"),
        P("dp", "tensor"),
        P(("tensor", "dp")),
        P("tensor", "dp"),
    )
    return jax.shard_map(
        per_device, mesh=mesh, in_specs=in_specs, out_specs=out_specs, check_vma=False
    )
```

profile of v0, /device:TPU:0, one launch (start us, length us, event | category | flops | bytes accessed | tf_op | source)
XLA Modules:
  0.0 1075.0 jit_solution(16801075878062956087)
XLA Ops:
  12.5 13.6 %all-gather.5 = bf16[8,1,256]{2,1,0:T(2,128)(2,1)S(1)} all-gather(bf16[1,1,256]{2,1,0:T(2,128)(2,1)S(1)} %reshape.282), channel_id=1, replica_groups=mesh['dp'=8,'tensor'=4] {'dp'}, dimensions={0}, use_global_device_ids=true | all-gather | bytes 4608 | tf_op jit(solution)/shard_map/all_gather | solution.py:64
  26.7 9.0 all-gather.4
  36.3 10.3 all-gather.3
  46.6 8.8 all-gather.1
  55.4 10.4 all-gather
  65.9 17.9 %all-gather.2 = bf16[8,64,3]{1,2,0:T(4,128)(2,1)S(1)} all-gather(bf16[1,64,3]{1,2,0:T(4,128)(2,1)S(1)} %bitcast.120), channel_id=1, replica_groups=mesh['dp'=8,'tensor'=4] {'dp'}, dimensions={0}, use_global_device_ids=true | all-gather | bytes 3456 | tf_op jit(solution)/shard_map/all_gather | solution.py:63
  92.0 17.6 %all-gather.12.cloned.1.call-done = bf16[3,2048,512]{1,2,0:T(8,128)(2,1)} async-done(((bf16[3,256,512]{1,2,0:T(8,128)(2,1)}), bf16[3,2048,512]{1,2,0:T(8,128)(2,1)}) %all-gather.12.cloned.1.call-update) | async-done | bytes 6291472 | tf_op jit(solution)/shard_map/all_gather | solution.py:59
  161.2 30.2 %all-gather.16.cloned.1.call-done = bf16[2048,2048]{1,0:T(8,128)(2,1)} async-done(((bf16[256,2048]{1,0:T(8,128)(2,1)}), bf16[2048,2048]{1,0:T(8,128)(2,1)}) %all-gather.16.cloned.1.call-update) | async-done | bytes 8388624 | tf_op jit(solution)/shard_map/all_gather | solution.py:61
  191.4 9.7 fusion.53
  201.1 72.7 %all-gather.18.cloned.1.call-done = bf16[2048,2048]{1,0:T(8,128)(2,1)} async-done(((bf16[2048,256]{1,0:T(8,128)(2,1)}), bf16[2048,2048]{1,0:T(8,128)(2,1)}) %all-gather.18.cloned.1.call-update) | async-done | bytes 8388624 | tf_op jit(solution)/shard_map/all_gather | solution.py:62
  273.9 10.8 %fusion.68 = (f32[2048]{0:T(1024)S(1)}, bf16[512,2048]{1,0:T(8,128)(2,1)}) fusion(f32[512,2048]{1,0:T(8,128)} %fusion.53, f32[2048]{0:T(1024)S(1)} %bitcast.114, bf16[2048,2048]{1,0:T(8,128)(2,1)} %all-gather.18.cloned.1.call-done, bf16[512,2048]{1,0:T(8,128)(2,1)} %param.27, f32[512]{0:T(512)S(1)} %copy-done.26), kind=kOutput, calls=%fused_computation.105 | convolution fusion | flops 4310693888 | bytes 16795648 | tf_op jit(solution)/shard_map/ld,fd->lf/dot_general | solution.py:148
  284.7 8.1 fusion.61
  292.8 7.8 fusion.40
  312.6 167.7 %all-reduce.6.cloned.1.call-done = (f32[512,2048]{1,0:T(8,128)}, f32[512,2048]{1,0:T(8,128)}) async-done(((f32[512,2048]{1,0:T(8,128)}, f32[512,2048]{1,0:T(8,128)}), (f32[512,2048]{1,0:T(8,128)}, f32[512,2048]{1,0:T(8,128)})) %all-reduce.6.cloned.1.call-update) | async-done | bytes 8388624 | tf_op jit(solution)/shard_map/psum | solution.py:140
  487.8 8.4 convolution_bitcast_fusion
  502.3 13.3 %fusion.55 = f32[2048,2048]{1,0:T(8,128)} fusion(bf16[512,2048]{1,0:T(8,128)(2,1)} %param.27, f32[512]{0:T(512)S(1)} %copy-done.26, f32[512,2048]{1,0:T(8,128)} %fusion.53, f32[2048]{0:T(1024)S(1)} %bitcast.116), kind=kOutput, calls=%fused_computation.96 | convolution fusion | flops 4304404480 | bytes 23078912 | tf_op jit(solution)/shard_map/lf,ld->fd/dot_general | solution.py:147
  515.7 10.0 fusion.38
  526.3 11.8 %all-gather.6 = bf16[8,1,256]{2,1,0:T(2,128)(2,1)S(1)} all-gather(bf16[1,1,256]{2,1,0:T(2,128)(2,1)S(1)} %reshape.284), channel_id=1, replica_groups=mesh['dp'=8,'tensor'=4] {'dp'}, dimensions={0}, use_global_device_ids=true | all-gather | bytes 4608 | tf_op jit(solution)/shard_map/all_gather | solution.py:65
  547.8 27.4 %all-reduce.2 = (f32[2048]{0:T(1024)S(1)}, f32[2048]{0:T(1024)S(1)}) all-reduce(f32[2048]{0:T(1024)S(1)} %get-tuple-element.141, f32[2048]{0:T(1024)S(1)} %get-tuple-element.173), channel_id=6, replica_groups=mesh['dp'=8,'tensor'=4] {'dp'}, use_global_device_ids=true, to_apply=%region_19.20.clone | all-reduce | flops 4096 | bytes 32768
  577.5 9.5 psum.24
  587.6 90.5 %reduce-scatter.11.cloned.1.call-done = f32[3,256,512]{1,2,0:T(8,128)} async-done(((f32[3,2048,512]{1,2,0:T(8,128)}), f32[3,256,512]{1,2,0:T(8,128)}) %reduce-scatter.11.cloned.1.call-update) | async-done | bytes 1572880 | tf_op jit(solution)/shard_map/reduce_scatter | solution.py:211
  681.1 48.0 %reduce-scatter.13.cloned.1.call-done = f32[512,256]{1,0:T(8,128)} async-done(((f32[512,2048]{1,0:T(8,128)}), f32[512,256]{1,0:T(8,128)}) %reduce-scatter.13.cloned.1.call-update) | async-done | bytes 524304 | tf_op jit(solution)/shard_map/reduce_scatter | solution.py:212
  729.1 169.5 %reduce-scatter.17.cloned.1.call-done = f32[2048,256]{1,0:T(8,128)} async-done(((f32[2048,2048]{1,0:T(8,128)}), f32[2048,256]{1,0:T(8,128)}) %reduce-scatter.17.cloned.1.call-update) | async-done | bytes 2097168 | tf_op jit(solution)/shard_map/reduce_scatter | solution.py:214
  898.6 169.6 %reduce-scatter.15.cloned.1.call-done = f32[256,2048]{1,0:T(8,128)} async-done(((f32[2048,2048]{1,0:T(8,128)}), f32[256,2048]{1,0:T(8,128)}) %reduce-scatter.15.cloned.1.call-update) | async-done | bytes 2097168 | tf_op jit(solution)/shard_map/reduce_scatter | solution.py:213
  (188 shorter events, 106.4 us)
Async XLA Ops:
  7.2 58.6 %copy-start.33 = (bf16[3,64]{1,0:T(4,128)(2,1)S(1)}, bf16[3,64]{1,0:T(4,128)(2,1)}, u32[]{:S(2)}) copy-start(bf16[3,64]{1,0:T(4,128)(2,1)} %param.34) | copy-start | bytes 1156
  7.2 76.6 %copy-start = (bf16[512,2048]{1,0:T(8,128)(2,1)S(1)}, bf16[512,2048]{1,0:T(8,128)(2,1)}, u32[]{:S(2)}) copy-start(bf16[512,2048]{1,0:T(8,128)(2,1)} %param.26) | copy-start | bytes 6291460
  7.3 80.3 %all-gather.14.cloned.1.call-start = ((), (), s32[]{:S(2)}) async-start(), calls=%async_computation.7 | async-start | bytes 2359296 | tf_op jit(solution)/shard_map/all_gather | solution.py:60
  8.0 101.5 %all-gather.12.cloned.1.call-start = ((), (), s32[]{:S(2)}) async-start(), calls=%async_computation.6 | async-start | bytes 7077888 | tf_op jit(solution)/shard_map/all_gather | solution.py:59
  10.3 181.1 %all-gather.16.cloned.1.call-start = ((), (), s32[]{:S(2)}) async-start(), calls=%async_computation.8 | async-start | bytes 9437184 | tf_op jit(solution)/shard_map/all_gather | solution.py:61
  11.1 262.8 %all-gather.18.cloned.1.call-start = ((), (), s32[]{:S(2)}) async-start(), calls=%async_computation.9 | async-start | bytes 9437184 | tf_op jit(solution)/shard_map/all_gather | solution.py:62
  11.7 468.6 %all-reduce.6.cloned.1.call-start = ((), (), s32[]{:S(2)}) async-start(), calls=%async_computation.16 | async-start | bytes 16777216 | tf_op jit(solution)/shard_map/psum | solution.py:140
  55.4 54.1 %copy-start.31 = (f32[8,1,256]{2,1,0:T(1,128)}, f32[8,1,256]{2,1,0:T(1,128)S(1)}, u32[]{:S(2)}) copy-start(f32[8,1,256]{2,1,0:T(1,128)S(1)} %convert_element_type.108) | copy-start | bytes 24580
  84.2 25.3 %copy-start.23 = (f32[512]{0:T(512)}, f32[512]{0:T(512)S(1)}, u32[]{:S(2)}) copy-start(f32[512]{0:T(512)S(1)} %broadcast_multiply_fusion.3) | copy-start | bytes 6148
  84.9 24.6 %copy-start.27 = (f32[512]{0:T(512)}, f32[512]{0:T(512)S(1)}, u32[]{:S(2)}) copy-start(f32[512]{0:T(512)S(1)} %add_rsqrt_fusion) | copy-start | bytes 6148
  151.0 40.4 %copy-start.24 = (f32[512]{0:T(512)S(1)}, f32[512]{0:T(512)}, u32[]{:S(2)}) copy-start(f32[512]{0:T(512)} %copy-done.23) | copy-start | bytes 6148
  151.0 40.4 %copy-start.28 = (f32[512]{0:T(512)S(1)}, f32[512]{0:T(512)}, u32[]{:S(2)}) copy-start(f32[512]{0:T(512)} %copy-done.27) | copy-start | bytes 6148
  151.0 40.4 %copy-start.29 = (f32[8,1,256]{2,1,0:T(1,128)S(1)}, f32[8,1,256]{2,1,0:T(1,128)}, u32[]{:S(2)}) copy-start(f32[8,1,256]{2,1,0:T(1,128)} %convert_element_type.111) | copy-start | bytes 24580
  191.4 82.4 %copy-start.26 = (f32[512]{0:T(512)S(1)}, f32[512]{0:T(512)}, u32[]{:S(2)}) copy-start(f32[512]{0:T(512)} %copy-done.25) | copy-start | bytes 6148
  191.4 82.4 %copy-start.30 = (f32[8,1,256]{2,1,0:T(1,128)S(1)}, f32[8,1,256]{2,1,0:T(1,128)}, u32[]{:S(2)}) copy-start(f32[8,1,256]{2,1,0:T(1,128)} %convert_element_type.112) | copy-start | bytes 24580
  273.9 30.1 %slice-start = ((s8[6291456]{0:T(1024)(128)(4,1)}), s8[4194304]{0:T(1024)(128)(4,1)S(1)}, s32[]{:S(2)}) async-start(s8[6291456]{0:T(1024)(128)(4,1)} %bitcast.82), calls=%async_computation.17 | async-start | bytes 8388608
  284.7 19.3 %slice-start.1 = ((s8[6291456]{0:T(1024)(128)(4,1)}), s8[2097152]{0:T(1024)(128)(4,1)S(1)}, s32[]{:S(2)}) async-start(s8[6291456]{0:T(1024)(128)(4,1)} %bitcast.82), calls=%async_computation.18 | async-start | bytes 4194304
  309.8 229.6 %reduce-scatter.19.cloned.1.call-start = ((), (), s32[]{:S(2)}) async-start(), calls=%async_computation.14 | async-start | bytes 294912
  312.5 264.0 %reduce-scatter.21.cloned.1.call-start = ((), (), s32[]{:S(2)}) async-start(), calls=%async_computation.15 | async-start | bytes 1179648
  487.8 190.3 %reduce-scatter.11.cloned.1.call-start = ((), (), s32[]{:S(2)}) async-start(), calls=%async_computation.10 | async-start | bytes 14155776 | tf_op jit(solution)/shard_map/reduce_scatter | solution.py:211
  496.2 232.9 %reduce-scatter.13.cloned.1.call-start = ((), (), s32[]{:S(2)}) async-start(), calls=%async_computation.11 | async-start | bytes 4718592 | tf_op jit(solution)/shard_map/reduce_scatter | solution.py:212
  502.2 396.4 %reduce-scatter.17.cloned.1.call-start = ((), (), s32[]{:S(2)}) async-start(), calls=%async_computation.13 | async-start | bytes 18874368 | tf_op jit(solution)/shard_map/reduce_scatter | solution.py:214
  515.6 552.5 %reduce-scatter.15.cloned.1.call-start = ((), (), s32[]{:S(2)}) async-start(), calls=%async_computation.12 | async-start | bytes 18874368 | tf_op jit(solution)/shard_map/reduce_scatter | solution.py:213
  525.7 12.5 %copy-start.40 = (u32[32]{0:T(128)S(1)}, u32[32]{0:T(128)}, u32[]{:S(2)}) copy-start(u32[32]{0:T(128)} %constant.135) | copy-start | bytes 388
  (31 other events, 130.7 us)
Sparse Core Ops, SparseCore 0:
  9.6 33.4 all-gather.13
  45.3 64.2 all-gather.11
  111.1 80.2 all-gather.15
  192.8 80.9 all-gather.17
  309.9 170.2 all-reduce.5
  482.9 31.4 reduce-scatter.18
  517.3 30.7 reduce-scatter.20
  550.4 127.6 reduce-scatter.10
  680.9 48.1 reduce-scatter.12
  731.9 166.6 reduce-scatter.16
  901.5 166.6 reduce-scatter.14
where the time goes:
time: 1080 us; the launch traced here: 1070 us
  waiting for transfers between devices  768 us (71%)
  blocking collectives  119 us (11%)
  matrix products  103 us (10%)
  local copies, waits for them, and re-layouts  44.3 us (4%)
  other arithmetic  24.7 us (2%)
  between operations  16.1 us (1%)
    reduce_scatter x1, waiting for transfers between devices, per_device(): lax.psum_scatter(dup_w, 'dp', scatter_dimension=0, tiled=True)  170 us
    reduce_scatter x1, waiting for transfers between devices, per_device(): lax.psum_scatter(ddown_w, 'dp', scatter_dimension=1, tiled=True)  169 us
    psum x1, waiting for transfers between devices, per_device(): branch_sum = lax.psum(attn_part + ffn_part, 'tensor')  168 us
    reduce_scatter x1, waiting for transfers between devices, per_device(): lax.psum_scatter(dqkv_w, 'dp', scatter_dimension=1, tiled=True)  90.5 us
    all_gather x1, waiting for transfers between devices, per_device(): lax.all_gather(down_weight, 'dp', axis=1, tiled=True)  72.7 us
    reduce_scatter x1, waiting for transfers between devices, per_device(): lax.psum_scatter(dout_w, 'dp', scatter_dimension=1, tiled=True)  48 us
    all_gather x1, waiting for transfers between devices, per_device(): lax.all_gather(up_weight, 'dp', axis=0, tiled=True)  30.2 us
    unnamed x1, blocking collectives  27.4 us
  transfers between devices with their start and end apart: 11, of which 8 were waited for; matrix products, arithmetic and copies ran while one was open for 12% of the time, Pallas kernels for 0%

commit v1 on v0

--- a/solution.py
+++ b/solution.py
@@ -137,7 +137,7 @@
     up_pre = jnp.dot(ffn_in, up_full, preferred_element_type=jnp.float32) + up_b.astype(jnp.float32)
     hidden = gelu_exact(up_pre).astype(jnp.bfloat16)
     ffn_part = jnp.dot(hidden, down_full, preferred_element_type=jnp.float32)
-    branch_sum = lax.psum(attn_part + ffn_part, "tensor")
+    branch_sum = jnp.sum(lax.all_gather(attn_part + ffn_part, "tensor"), axis=0)
     block_output = (x_rows + branch_sum + outb_full.astype(jnp.float32)).astype(jnp.bfloat16)
     qkv_back, out_back, up_back, down_back = (qkv_full, out_full, up_full, down_full)
     row_valid = (positions < seq_len).astype(jnp.float32)[:, None]

time: 1080 us -> 1160 us (1.074)
  waiting for transfers between devices: 768 us -> 835 us
    all_gather x0 -> x1, waiting for transfers between devices: none -> 155 us  [per_device(): branch_sum = jnp.sum(lax.all_gather(attn_part + ffn_part, 'tensor'), axis=0)]
    psum x1, waiting for transfers between devices: 168 us -> 99.3 us  [per_device(): norm_grad, stat_sum = lax.psum((norm_part, norm_stats), 'tensor')]
    reduce_scatter x1, waiting for transfers between devices: 48 us -> 4.96 us  [per_device(): lax.psum_scatter(dout_w, 'dp', scatter_dimension=1, tiled=True)]
    reduce_scatter x1, waiting for transfers between devices: 90.5 us -> 113 us  [per_device(): lax.psum_scatter(dqkv_w, 'dp', scatter_dimension=1, tiled=True)]
    unnamed x109 -> x105, local copies, waits for them, and re-layouts: 24.1 us -> 22.3 us
  transfers between devices with their start and end apart: 11 -> 12, of which waited for: 8 -> 9; matrix products, arithmetic and copies ran while one was open for 12% -> 13% of each run, Pallas kernels for 0% -> 0%
where the time goes in v1:
time: 1160 us; the launch traced here: 1150 us
  waiting for transfers between devices  835 us (72%)
  blocking collectives  121 us (10%)
  matrix products  104 us (9%)
  local copies, waits for them, and re-layouts  42.5 us (4%)
  other arithmetic  34.3 us (3%)
  between operations  16.3 us (1%)
    reduce_scatter x1, waiting for transfers between devices, per_device(): lax.psum_scatter(dup_w, 'dp', scatter_dimension=0, tiled=True)  170 us
    reduce_scatter x1, waiting for transfers between devices, per_device(): lax.psum_scatter(ddown_w, 'dp', scatter_dimension=1, tiled=True)  169 us
    all_gather x1, waiting for transfers between devices, per_device(): branch_sum = jnp.sum(lax.all_gather(attn_part + ffn_part, 'tensor'), axis=0)  155 us
    reduce_scatter x1, waiting for transfers between devices, per_device(): lax.psum_scatter(dqkv_w, 'dp', scatter_dimension=1, tiled=True)  113 us
    psum x1, waiting for transfers between devices, per_device(): norm_grad, stat_sum = lax.psum((norm_part, norm_stats), 'tensor')  99.3 us
    all_gather x1, waiting for transfers between devices, per_device(): lax.all_gather(down_weight, 'dp', axis=1, tiled=True)  72.8 us
    all_gather x1, waiting for transfers between devices, per_device(): lax.all_gather(up_weight, 'dp', axis=0, tiled=True)  31.5 us
    unnamed x1, blocking collectives  30.2 us
  transfers between devices with their start and end apart: 12, of which 9 were waited for; matrix products, arithmetic and copies ran while one was open for 13% of the time, Pallas kernels for 0%

profile of v1, /device:TPU:0, one launch (start us, length us, event | category | flops | bytes accessed | tf_op | source)
XLA Modules:
  0.0 1153.9 jit_solution(10238605082262000953)
XLA Ops:
  12.4 13.6 %all-gather.5 = bf16[8,1,256]{2,1,0:T(2,128)(2,1)S(1)} all-gather(bf16[1,1,256]{2,1,0:T(2,128)(2,1)S(1)} %reshape.281), channel_id=1, replica_groups=mesh['dp'=8,'tensor'=4] {'dp'}, dimensions={0}, use_global_device_ids=true | all-gather | bytes 4608 | tf_op jit(solution)/shard_map/all_gather | solution.py:69
  26.6 9.0 all-gather.4
  35.6 10.4 all-gather.6
  46.6 8.7 all-gather.1
  55.4 10.5 all-gather.3
  66.0 17.9 %all-gather.2 = bf16[8,1,256]{2,1,0:T(2,128)(2,1)S(1)} all-gather(bf16[1,1,256]{2,1,0:T(2,128)(2,1)S(1)} %reshape.275), channel_id=1, replica_groups=mesh['dp'=8,'tensor'=4] {'dp'}, dimensions={0}, use_global_device_ids=true | all-gather | bytes 4608 | tf_op jit(solution)/shard_map/all_gather | solution.py:67
  91.9 17.6 %all-gather.14.cloned.1.call-done = bf16[3,2048,512]{1,2,0:T(8,128)(2,1)} async-done(((bf16[3,256,512]{1,2,0:T(8,128)(2,1)}), bf16[3,2048,512]{1,2,0:T(8,128)(2,1)}) %all-gather.14.cloned.1.call-update) | async-done | bytes 6291472 | tf_op jit(solution)/shard_map/all_gather | solution.py:59
  159.9 31.5 %all-gather.18.cloned.1.call-done = bf16[2048,2048]{1,0:T(8,128)(2,1)} async-done(((bf16[256,2048]{1,0:T(8,128)(2,1)}), bf16[2048,2048]{1,0:T(8,128)(2,1)}) %all-gather.18.cloned.1.call-update) | async-done | bytes 8388624 | tf_op jit(solution)/shard_map/all_gather | solution.py:61
  191.5 9.6 fusion.53
  201.1 72.8 %all-gather.20.cloned.1.call-done = bf16[2048,2048]{1,0:T(8,128)(2,1)} async-done(((bf16[2048,256]{1,0:T(8,128)(2,1)}), bf16[2048,2048]{1,0:T(8,128)(2,1)}) %all-gather.20.cloned.1.call-update) | async-done | bytes 8388624 | tf_op jit(solution)/shard_map/all_gather | solution.py:62
  273.9 9.9 fusion.68
  288.4 10.3 fusion.27
  301.4 99.3 %all-reduce.5.cloned.1.call-done = f32[512,2048]{1,0:T(8,128)} async-done(((f32[512,2048]{1,0:T(8,128)}), f32[512,2048]{1,0:T(8,128)}) %all-reduce.5.cloned.1.call-update) | async-done | bytes 4194320 | tf_op jit(solution)/shard_map/psum | solution.py:204
  416.9 9.3 fusion.61
  434.7 10.0 fusion.38
  444.9 13.4 %fusion.55 = f32[2048,2048]{1,0:T(8,128)} fusion(bf16[512,2048]{1,0:T(8,128)(2,1)} %param.27, f32[512]{0:T(512)S(1)} %copy-done.25, f32[512,2048]{1,0:T(8,128)} %fusion.53, f32[2048]{0:T(1024)S(1)} %bitcast.114), kind=kOutput, calls=%fused_computation.96 | convolution fusion | flops 4304404480 | bytes 23078912 | tf_op jit(solution)/shard_map/lf,ld->fd/dot_general | solution.py:147
  459.0 11.8 %all-gather.7 = bf16[8,1,256]{2,1,0:T(2,128)(2,1)S(1)} all-gather(bf16[1,1,256]{2,1,0:T(2,128)(2,1)S(1)} %reshape.285), channel_id=1, replica_groups=mesh['dp'=8,'tensor'=4] {'dp'}, dimensions={0}, use_global_device_ids=true | all-gather | bytes 4608 | tf_op jit(solution)/shard_map/all_gather | solution.py:65
  474.5 8.9 psum.16
  484.0 112.9 %reduce-scatter.11.cloned.1.call-done = f32[3,256,512]{1,2,0:T(8,128)} async-done(((f32[3,2048,512]{1,2,0:T(8,128)}), f32[3,256,512]{1,2,0:T(8,128)}) %reduce-scatter.11.cloned.1.call-update) | async-done | bytes 1572880 | tf_op jit(solution)/shard_map/reduce_scatter | solution.py:211
  599.9 154.6 %all-gather.22.cloned.1.call-done = f32[2048,2048]{1,0:T(8,128)} async-done(((f32[512,2048]{1,0:T(8,128)}), f32[2048,2048]{1,0:T(8,128)}) %all-gather.22.cloned.1.call-update) | async-done | bytes 16777232 | tf_op jit(solution)/shard_map/all_gather | solution.py:140
  754.5 10.2 reduce_sum.120
  771.4 30.2 %all-reduce.2 = (f32[2048]{0:T(1024)S(1)}, f32[2048]{0:T(1024)S(1)}) all-reduce(f32[2048]{0:T(1024)S(1)} %get-tuple-element.139, f32[2048]{0:T(1024)S(1)} %get-tuple-element.171), channel_id=7, replica_groups=mesh['dp'=8,'tensor'=4] {'dp'}, use_global_device_ids=true, to_apply=%region_19.20.clone | all-reduce | flops 4096 | bytes 32768
  807.8 169.6 %reduce-scatter.15.cloned.1.call-done = f32[256,2048]{1,0:T(8,128)} async-done(((f32[2048,2048]{1,0:T(8,128)}), f32[256,2048]{1,0:T(8,128)}) %reduce-scatter.15.cloned.1.call-update) | async-done | bytes 2097168 | tf_op jit(solution)/shard_map/reduce_scatter | solution.py:213
  977.4 169.5 %reduce-scatter.17.cloned.1.call-done = f32[2048,256]{1,0:T(8,128)} async-done(((f32[2048,2048]{1,0:T(8,128)}), f32[2048,256]{1,0:T(8,128)}) %reduce-scatter.17.cloned.1.call-update) | async-done | bytes 2097168 | tf_op jit(solution)/shard_map/reduce_scatter | solution.py:214
  (187 shorter events, 116.3 us)
Async XLA Ops:
  7.2 28.4 %copy-start.36 = (bf16[256]{0:T(256)(128)(2,1)S(1)}, bf16[256]{0:T(256)(128)(2,1)}, u32[]{:S(2)}) copy-start(bf16[256]{0:T(256)(128)(2,1)} %param.38) | copy-start | bytes 1540
  7.2 39.4 %copy-start.37 = (bf16[256]{0:T(256)(128)(2,1)S(1)}, bf16[256]{0:T(256)(128)(2,1)}, u32[]{:S(2)}) copy-start(bf16[256]{0:T(256)(128)(2,1)} %param.29) | copy-start | bytes 1540
  7.2 48.2 %copy-start.32 = (bf16[3,64]{1,0:T(4,128)(2,1)S(1)}, bf16[3,64]{1,0:T(4,128)(2,1)}, u32[]{:S(2)}) copy-start(bf16[3,64]{1,0:T(4,128)(2,1)} %param.34) | copy-start | bytes 1156
  7.2 58.7 %copy-start.38 = (bf16[256]{0:T(256)(128)(2,1)S(1)}, bf16[256]{0:T(256)(128)(2,1)}, u32[]{:S(2)}) copy-start(bf16[256]{0:T(256)(128)(2,1)} %param.30) | copy-start | bytes 1540
  7.2 76.6 %copy-start = (bf16[512,2048]{1,0:T(8,128)(2,1)S(1)}, bf16[512,2048]{1,0:T(8,128)(2,1)}, u32[]{:S(2)}) copy-start(bf16[512,2048]{1,0:T(8,128)(2,1)} %param.26) | copy-start | bytes 6291460
  7.3 80.3 %all-gather.16.cloned.1.call-start = ((), (), s32[]{:S(2)}) async-start(), calls=%async_computation.7 | async-start | bytes 2359296 | tf_op jit(solution)/shard_map/all_gather | solution.py:60
  8.0 101.5 %all-gather.14.cloned.1.call-start = ((), (), s32[]{:S(2)}) async-start(), calls=%async_computation.6 | async-start | bytes 7077888 | tf_op jit(solution)/shard_map/all_gather | solution.py:59
  10.3 181.1 %all-gather.18.cloned.1.call-start = ((), (), s32[]{:S(2)}) async-start(), calls=%async_computation.8 | async-start | bytes 9437184 | tf_op jit(solution)/shard_map/all_gather | solution.py:61
  11.1 262.8 %all-gather.20.cloned.1.call-start = ((), (), s32[]{:S(2)}) async-start(), calls=%async_computation.9 | async-start | bytes 9437184 | tf_op jit(solution)/shard_map/all_gather | solution.py:62
  11.7 389.0 %all-reduce.5.cloned.1.call-start = ((), (), s32[]{:S(2)}) async-start(), calls=%async_computation.10 | async-start | bytes 8388608 | tf_op jit(solution)/shard_map/psum | solution.py:204
  83.8 25.7 %copy-start.30 = (f32[8,1,256]{2,1,0:T(1,128)}, f32[8,1,256]{2,1,0:T(1,128)S(1)}, u32[]{:S(2)}) copy-start(f32[8,1,256]{2,1,0:T(1,128)S(1)} %convert_element_type.108) | copy-start | bytes 24580
  84.2 25.3 %copy-start.22 = (f32[512]{0:T(512)}, f32[512]{0:T(512)S(1)}, u32[]{:S(2)}) copy-start(f32[512]{0:T(512)S(1)} %broadcast_multiply_fusion.3) | copy-start | bytes 6148
  149.7 41.7 %copy-start.23 = (f32[512]{0:T(512)S(1)}, f32[512]{0:T(512)}, u32[]{:S(2)}) copy-start(f32[512]{0:T(512)} %copy-done.22) | copy-start | bytes 6148
  149.7 41.7 %copy-start.27 = (f32[512]{0:T(512)S(1)}, f32[512]{0:T(512)}, u32[]{:S(2)}) copy-start(f32[512]{0:T(512)} %copy-done.26) | copy-start | bytes 6148
  149.7 41.7 %copy-start.29 = (f32[8,1,256]{2,1,0:T(1,128)S(1)}, f32[8,1,256]{2,1,0:T(1,128)}, u32[]{:S(2)}) copy-start(f32[8,1,256]{2,1,0:T(1,128)} %convert_element_type.111) | copy-start | bytes 24580
  191.4 82.4 %copy-start.25 = (f32[512]{0:T(512)S(1)}, f32[512]{0:T(512)}, u32[]{:S(2)}) copy-start(f32[512]{0:T(512)} %copy-done.24) | copy-start | bytes 6148
  191.4 82.4 %copy-start.28 = (f32[8,1,256]{2,1,0:T(1,128)S(1)}, f32[8,1,256]{2,1,0:T(1,128)}, u32[]{:S(2)}) copy-start(f32[8,1,256]{2,1,0:T(1,128)} %convert_element_type.112) | copy-start | bytes 24580
  298.7 173.4 %reduce-scatter.19.cloned.1.call-start = ((), (), s32[]{:S(2)}) async-start(), calls=%async_computation.16 | async-start | bytes 294912
  301.4 172.1 %reduce-scatter.21.cloned.1.call-start = ((), (), s32[]{:S(2)}) async-start(), calls=%async_computation.17 | async-start | bytes 1179648
  408.1 188.8 %reduce-scatter.11.cloned.1.call-start = ((), (), s32[]{:S(2)}) async-start(), calls=%async_computation.11 | async-start | bytes 14155776 | tf_op jit(solution)/shard_map/reduce_scatter | solution.py:211
  416.9 337.7 %all-gather.22.cloned.1.call-start = ((), (), s32[]{:S(2)}) async-start(), calls=%async_computation.15 | async-start | bytes 20971520 | tf_op jit(solution)/shard_map/all_gather | solution.py:140
  429.7 378.1 %reduce-scatter.13.cloned.1.call-start = ((), (), s32[]{:S(2)}) async-start(), calls=%async_computation.12 | async-start | bytes 4718592 | tf_op jit(solution)/shard_map/reduce_scatter | solution.py:212
  434.7 542.7 %reduce-scatter.15.cloned.1.call-start = ((), (), s32[]{:S(2)}) async-start(), calls=%async_computation.13 | async-start | bytes 18874368 | tf_op jit(solution)/shard_map/reduce_scatter | solution.py:213
  444.7 702.2 %reduce-scatter.17.cloned.1.call-start = ((), (), s32[]{:S(2)}) async-start(), calls=%async_computation.14 | async-start | bytes 18874368 | tf_op jit(solution)/shard_map/reduce_scatter | solution.py:214
  (30 other events, 180.7 us)
Sparse Core Ops, SparseCore 0:
  9.6 33.4 all-gather.15
  45.3 64.2 all-gather.13
  111.1 80.2 all-gather.17
  192.9 80.9 all-gather.19
  298.8 101.8 all-reduce.4
  402.8 30.8 reduce-scatter.18
  436.5 30.7 reduce-scatter.20
  469.6 127.2 reduce-scatter.10
  598.7 155.7 all-gather.21
  757.3 50.5 reduce-scatter.12
  810.7 166.6 reduce-scatter.14
  980.2 166.6 reduce-scatter.16
